TPU v7x, 512 devices: a whole 4x8x8 slice. The times are simulated.
512 devices in a mesh: gx: 8 (over z_lo, core), gy: 8 (over y), gz: 8 (over x, z_hi).
Axes of the slice: x: 4, y: 8, z: 8 (z_hi: 2, z_lo: 4; z = z_hi * 4 + z_lo), core: 2. Of those that a mesh axis runs over, the one named last changes fastest.
Arguments:
- right_side: float32 [131072, 2048], P(('gx', 'gy'), 'gz'), may hold values from -6 to 6
- send_order: int32 [64, 2048], P(('gx', 'gy')), may hold values from 0 to 2047, each once within a row
- recv_order: int32 [64, 2048], P(('gx', 'gy')), may hold values from 0 to 2047, each once within a row
- update_target: int32 [256, 2], P('gx'), may hold values from 0 to 63, as said below
- leaf_inv: float32 [256, 256, 256], P(('gx', 'gy'), 'gz'), may hold values from -0.375 to 0.375
- leaf_low: float32 [256, 256, 256], P(('gx', 'gy'), 'gz'), may hold values from -0.375 to 0.375
- parent_inv: float32 [128, 512, 512], P(('gx', 'gy'), 'gz'), may hold values from -0.25 to 0.25
Outputs:
- solution: float32 [131072, 2048], P(('gx', 'gy'), 'gz')
Inputs may be any that keep to these rules, and one draw needn't show every extreme that they name: `update_target`: entries are 4 * parent + block, with parent counted among the 2 * 8 parents of the leaf's gx index and block below 4; a leaf's two entries name the same parent and two different blocks. Among the 4 leaves of one index of gx+gy, at most 1 name parents held by one index of gy (parent // 2), and exactly 1 do so for some index of gy.
All inputs are finite; a program needn't handle non-finite values.
Results may differ from a plain program's by a relative error of at most 0.000073.
Values sent between devices are 32-bit elements; how exact they have to be, the bound alone decides.
A program may use at most 64 MiB of HBM per device.

v0:
```python
import jax
import jax.numpy as jnp
from jax import lax
from jax.sharding import PartitionSpec as P

PIV = 256
BLK = 128
LEAF_DEV = 4
PAR_DEV = 2


def cut_along(x, dim, size):
    before, after = (x.shape[:dim], x.shape[dim + 1 :])
    return jnp.moveaxis(x.reshape(*before, size, -1, *after), dim, 0)


def piece_ends(length, count):
    lap = length // count
    if lap >= 8:
        lap -= lap % 8
    return [lap * k for k in range(1, count)]


def in_order(parts, dim):
    shape = list(parts.shape[1:])
    shape[dim] *= parts.shape[0]
    return jnp.moveaxis(parts, 0, dim).reshape(shape)


def several_exchanges(x, axis, pieces, split_dim, concat_dim):
    parts = cut_along(x, split_dim, lax.axis_size(axis))
    split_at = max(range(1, max(2, parts.ndim - 1)), key=lambda d: parts.shape[d])
    finished = []
    for share in jnp.split(parts, piece_ends(parts.shape[split_at], pieces), axis=split_at):
        if share.size:
            finished.append(lax.all_to_all(share, axis, split_axis=0, concat_axis=0, tiled=True))
    return in_order(jnp.concatenate(finished, axis=split_at), concat_dim)


def side_by_side(arrays, axis, dim, along):
    ends, at = ([], 0)
    for a in arrays[:-1]:
        at += a.shape[along]
        ends.append(at)
    both = jnp.concatenate(arrays, axis=along)
    return tuple(jnp.split(lax.all_gather(both, axis, axis=dim, tiled=True), ends, axis=along))


def body(right_side, send_order, recv_order, update_target, leaf_inv, leaf_low, parent_inv):
    columns = right_side.shape[1]
    outgoing = jnp.take(right_side, send_order[0], axis=0)
    arrived = several_exchanges(outgoing, ("gx", "gy"), 2, 0, 0)
    front_rows = jnp.take(arrived, recv_order[0], axis=0)
    leaf_rhs = front_rows[: LEAF_DEV * PIV].reshape(LEAF_DEV, PIV, columns)
    parent_rhs = front_rows[LEAF_DEV * PIV :].reshape(PAR_DEV, 4 * BLK, columns)
    inv_whole, low_whole = side_by_side((leaf_inv, leaf_low), "gz", 1, 0)
    leaf_sol = jnp.einsum("lij,ljc->lic", inv_whole, leaf_rhs, precision=lax.Precision.HIGHEST)
    update = jnp.einsum("lij,ljc->lic", low_whole, leaf_sol, precision=lax.Precision.HIGHEST)
    gy_count = lax.axis_size("gy")
    gy_index = lax.axis_index("gy")
    own_blocks = PAR_DEV * 4
    base_block = gy_index * own_blocks
    block_iota = jnp.arange(own_blocks, dtype=jnp.int32)
    capacity = (LEAF_DEV + gy_count - 1) // gy_count
    owner_index = (update_target[:, 0] // 4 // PAR_DEV).reshape(gy_count, LEAF_DEV)
    leaf_iota = jnp.arange(LEAF_DEV, dtype=jnp.int32)
    earlier = leaf_iota[None, :] < leaf_iota[:, None]
    same_owner = owner_index[:, :, None] == owner_index[:, None, :]
    slot_rank = jnp.sum((same_owner & earlier[None]).astype(jnp.int32), axis=2)
    slot_iota = jnp.arange(gy_count * capacity, dtype=jnp.int32)
    own_target = lax.dynamic_index_in_dim(owner_index, gy_index, 0, keepdims=False)
    own_rank = lax.dynamic_index_in_dim(slot_rank, gy_index, 0, keepdims=False)
    packing = (slot_iota[:, None] == (own_target * capacity + own_rank)[None, :]).astype(
        jnp.float32
    )
    sending = jnp.einsum("kl,lrc->krc", packing, update, precision=lax.Precision.HIGHEST)
    received = lax.all_to_all(sending, "gy", split_axis=0, concat_axis=0, tiled=True)
    source_iota = jnp.arange(gy_count, dtype=jnp.int32)[:, None]
    slot_index = (source_iota * capacity + slot_rank).reshape(-1)
    present = (owner_index == gy_index).reshape(-1)
    matched = (present[:, None] & (slot_index[:, None] == slot_iota[None, :])).astype(jnp.float32)
    local_block = update_target - base_block
    chosen = (local_block[:, :, None] == block_iota[None, None, :]).astype(jnp.float32)
    placing = jnp.einsum("lk,ljb->bkj", matched, chosen, precision=lax.Precision.HIGHEST)
    placing = placing.reshape(own_blocks, gy_count * capacity * 2)
    incoming = received.reshape(gy_count * capacity * 2, BLK, columns)
    contribution = jnp.einsum("bm,mrc->brc", placing, incoming, precision=lax.Precision.HIGHEST)
    reduced = parent_rhs - contribution.reshape(PAR_DEV, 4 * BLK, columns)
    parent_sol = jnp.einsum(
        "pij,pjc->pic",
        lax.all_gather(parent_inv, "gz", axis=1, tiled=True),
        reduced,
        precision=lax.Precision.HIGHEST,
    )
    return jnp.concatenate([leaf_sol.reshape(-1, columns), parent_sol.reshape(-1, columns)], axis=0)


def solution(mesh):
    placed = (
        P(("gx", "gy"), "gz"),
        P(("gx", "gy"), None),
        P(("gx", "gy"), None),
        P("gx", None),
        P(("gx", "gy"), "gz", None),
        P(("gx", "gy"), "gz", None),
        P(("gx", "gy"), "gz", None),
    )
    return jax.shard_map(
        body, mesh=mesh, in_specs=placed, out_specs=P(("gx", "gy"), "gz"), check_vma=False
    )
```

profile of v0, /device:TPU:1, one launch (start us, length us, event | category | flops | bytes accessed | tf_op | source)
XLA Modules:
  0.0 254.7 jit_solution(5999290325724774444)
XLA Ops:
  6.5 0.0 copy-start
  6.5 0.9 fusion.4
  7.4 0.7 compare_and_fusion.1
  8.1 0.1 copy-done
  8.1 8.6 %gather_fusion = f32[2048,256]{1,0:T(8,128)} fusion(f32[2048,256]{1,0:T(8,128)S(1)} %copy-done, s32[2048]{0:T(1024)S(1)} %fusion.4), kind=kCustom, calls=%fused_computation.clone | custom fusion | bytes 4202496 | tf_op jit(solution)/shard_map/jit(_take)/gather | solution.py:51
  16.7 1.9 broadcast_select_fusion.1
  18.7 1.5 fusion.20
  20.2 14.7 %all-to-all-start = ((f32[64,16,256]{2,1,0:T(8,128)}), f32[64,16,256]{2,1,0:T(8,128)S(1)}, u32[]{:S(2)}, u32[]{:S(2)}) async-start(f32[64,16,256]{2,1,0:T(8,128)} %get-tuple-element.8), calls=%async_computation | async-start | bytes 2097152 | tf_op jit(solution)/shard_map/all_to_all | solution.py:36
  34.9 0.0 all-gather.3.cloned.1.call-start
  35.0 0.0 copy-done.3
  35.0 0.0 copy-done.4
  35.0 0.7 pad_maximum_fusion.2
  35.7 0.0 all-gather.3.cloned.1.call-update
  35.7 28.0 %all-to-all-done = f32[64,16,256]{2,1,0:T(8,128)S(1)} async-done(((f32[64,16,256]{2,1,0:T(8,128)}), f32[64,16,256]{2,1,0:T(8,128)S(1)}, u32[]{:S(2)}, u32[]{:S(2)}) %all-to-all-start) | async-done | bytes 1048608 | tf_op jit(solution)/shard_map/all_to_all | solution.py:36
  63.8 6.2 %all-to-all-start.1 = ((f32[64,16,256]{2,1,0:T(8,128)}), f32[64,16,256]{2,1,0:T(8,128)}, u32[]{:S(2)}, u32[]{:S(2)}) async-start(f32[64,16,256]{2,1,0:T(8,128)} %get-tuple-element.9), calls=%async_computation.1 | async-start | bytes 2097152 | tf_op jit(solution)/shard_map/all_to_all | solution.py:36
  69.9 0.0 copy-done.6
  70.0 0.1 squeeze.14
  70.0 0.1 copy.39
  70.1 0.1 convert_reduce_fusion
  70.2 0.2 add_reduce_fusion
  70.4 0.0 copy-done.5
  70.5 28.5 %all-to-all-done.1 = f32[64,16,256]{2,1,0:T(8,128)} async-done(((f32[64,16,256]{2,1,0:T(8,128)}), f32[64,16,256]{2,1,0:T(8,128)}, u32[]{:S(2)}, u32[]{:S(2)}) %all-to-all-start.1) | async-done | bytes 1048608 | tf_op jit(solution)/shard_map/all_to_all | solution.py:36
  99.0 2.8 %pad_maximum_fusion = f32[64,32,256]{2,1,0:T(8,128)} fusion(f32[64,16,256]{2,1,0:T(8,128)} %all-to-all-done.1, f32[64,16,256]{2,1,0:T(8,128)S(1)} %all-to-all-done), kind=kLoop, calls=%fused_computation.2 | loop fusion | flops 524288 | bytes 4194304 | tf_op jit(solution)/shard_map/concatenate | solution.py:37
  101.8 10.2 %gather_fusion.1 = f32[2048,256]{1,0:T(8,128)} fusion(f32[2048,256]{1,0:T(8,128)} %bitcast.34, s32[2048]{0:T(1024)S(1)} %fusion.5), kind=kCustom, calls=%fused_computation.1.clone | custom fusion | bytes 4202496 | tf_op jit(solution)/shard_map/jit(_take)/gather | solution.py:53
  111.9 1.9 broadcast_select_fusion
  113.9 1.4 fusion.19
  115.3 15.8 %all-gather.3.cloned.1.call-done = f32[8,256,256]{2,1,0:T(8,128)} async-done(((f32[8,32,256]{2,1,0:T(8,128)}), f32[8,256,256]{2,1,0:T(8,128)}) %all-gather.3.cloned.1.call-update) | async-done | bytes 2097168 | tf_op jit(solution)/shard_map/all_gather | solution.py:46
  131.1 2.8 %fusion.21 = f32[4,256,256]{2,1,0:T(8,128)S(1)} fusion(f32[8,256,256]{2,1,0:T(8,128)} %all-gather.3.cloned.1.call-done, f32[4,256,256]{2,1,0:T(8,128)} %bitcast.40), kind=kOutput, calls=%fused_computation.61 | convolution fusion | flops 805306368 | bytes 4194304 | tf_op jit(solution)/shard_map/lij,ljc->lic/dot_general | solution.py:57
  134.0 0.0 copy-done.1
  134.0 1.1 fusion.22
  135.1 1.9 fusion.2
  137.1 2.0 copy.46
  139.0 5.7 %all-to-all-start.2 = ((f32[8,256,256]{2,1,0:T(8,128)}), f32[8,256,256]{2,1,0:T(8,128)}, u32[]{:S(2)}, u32[]{:S(2)}) async-start(f32[8,256,256]{2,1,0:T(8,128)} %copy.46), calls=%async_computation.2 | async-start | bytes 4194304 | tf_op jit(solution)/shard_map/all_to_all | solution.py:77
  144.8 0.2 all-gather.5.cloned.1.call-start
  145.0 0.5 all-gather.5.cloned.1.call-update
  145.5 0.1 copy.43
  145.6 0.1 add.56
  145.7 0.1 convolution_bitcast_fusion.1
  145.9 0.1 copy.44
  145.9 50.6 %all-to-all-done.2 = f32[8,256,256]{2,1,0:T(8,128)} async-done(((f32[8,256,256]{2,1,0:T(8,128)}), f32[8,256,256]{2,1,0:T(8,128)}, u32[]{:S(2)}, u32[]{:S(2)}) %all-to-all-start.2) | async-done | bytes 2097184 | tf_op jit(solution)/shard_map/all_to_all | solution.py:77
  196.5 3.9 %fusion = f32[8,128,256]{2,0,1:T(8,128)S(1)} fusion(f32[8,16,1]{0,1,2:T(8,128)S(1)} %bitcast.41, f32[16,128,256]{2,1,0:T(8,128)} %bitcast.13), kind=kOutput, calls=%fused_computation.4 | convolution fusion | flops 50331648 | bytes 3146240 | tf_op jit(solution)/shard_map/bm,mrc->brc/dot_general | solution.py:87
  200.4 0.3 copy.49
  200.8 0.0 copy-done.2
  200.8 1.1 bitcast_subtract_fusion
  201.9 34.3 %all-gather.5.cloned.1.call-done = f32[2,512,512]{2,1,0:T(8,128)} async-done(((f32[2,64,512]{2,1,0:T(8,128)}), f32[2,512,512]{2,1,0:T(8,128)}) %all-gather.5.cloned.1.call-update) | async-done | bytes 2097168 | tf_op jit(solution)/shard_map/all_gather | solution.py:91
  236.2 6.4 %convolution_bitcast_fusion = f32[2,512,256]{1,2,0:T(8,128)} fusion(f32[2,512,256]{2,1,0:T(8,128)} %bitcast_subtract_fusion, f32[2,512,512]{2,1,0:T(8,128)} %all-gather.5.cloned.1.call-done), kind=kOutput, calls=%fused_computation.6 | convolution fusion | flops 1610612736 | bytes 4194304 | tf_op jit(solution)/shard_map/pij,pjc->pic/dot_general | solution.py:89
  242.6 2.5 copy.51
  245.1 2.7 %pad_maximum_fusion.1 = f32[2048,256]{1,0:T(8,128)} fusion(f32[1024,256]{1,0:T(8,128)} %bitcast.39, f32[1024,256]{1,0:T(8,128)S(1)} %bitcast.35), kind=kLoop, calls=%fused_computation.3 | loop fusion | flops 524288 | bytes 4194304 | tf_op jit(solution)/shard_map/concatenate | solution.py:95
  (14 shorter events, 0.1 us)
Async XLA Ops:
  6.5 1.6 copy-start
  20.2 14.8 %copy-start.3 = (f32[4,32,256]{2,1,0:T(8,128)S(1)}, f32[4,32,256]{2,1,0:T(8,128)}, u32[]{:S(2)}) copy-start(f32[4,32,256]{2,1,0:T(8,128)} %param.14) | copy-start | bytes 393220
  20.2 14.8 %copy-start.4 = (f32[4,32,256]{2,1,0:T(8,128)S(1)}, f32[4,32,256]{2,1,0:T(8,128)}, u32[]{:S(2)}) copy-start(f32[4,32,256]{2,1,0:T(8,128)} %param.13) | copy-start | bytes 393220
  20.2 49.8 %copy-start.6 = (s32[32,2]{0,1:T(2,128)S(1)}, s32[32,2]{0,1:T(2,128)}, u32[]{:S(2)}) copy-start(s32[32,2]{0,1:T(2,128)} %param.12) | copy-start | bytes 772
  20.2 50.3 %copy-start.5 = (s32[1,2048]{1,0:T(1,128)S(1)}, s32[1,2048]{1,0:T(1,128)}, u32[]{:S(2)}) copy-start(s32[1,2048]{1,0:T(1,128)} %param.11) | copy-start | bytes 24580
  20.2 43.6 %all-to-all-start = ((f32[64,16,256]{2,1,0:T(8,128)}), f32[64,16,256]{2,1,0:T(8,128)S(1)}, u32[]{:S(2)}, u32[]{:S(2)}) async-start(f32[64,16,256]{2,1,0:T(8,128)} %get-tuple-element.8), calls=%async_computation | async-start | bytes 2097152 | tf_op jit(solution)/shard_map/all_to_all | solution.py:36
  34.9 96.2 %all-gather.3.cloned.1.call-start = ((), (), s32[]{:S(2)}) async-start(), calls=%async_computation.3 | async-start | bytes 2359296 | tf_op jit(solution)/shard_map/all_gather | solution.py:46
  63.8 35.3 %all-to-all-start.1 = ((f32[64,16,256]{2,1,0:T(8,128)}), f32[64,16,256]{2,1,0:T(8,128)}, u32[]{:S(2)}, u32[]{:S(2)}) async-start(f32[64,16,256]{2,1,0:T(8,128)} %get-tuple-element.9), calls=%async_computation.1 | async-start | bytes 2097152 | tf_op jit(solution)/shard_map/all_to_all | solution.py:36
  131.1 2.8 %copy-start.1 = (f32[8,256,256]{2,1,0:T(8,128)S(1)}, f32[8,256,256]{2,1,0:T(8,128)}, u32[]{:S(2)}) copy-start(f32[8,256,256]{2,1,0:T(8,128)} %all-gather.3.cloned.1.call-done) | copy-start | bytes 6291460
  139.0 57.5 %all-to-all-start.2 = ((f32[8,256,256]{2,1,0:T(8,128)}), f32[8,256,256]{2,1,0:T(8,128)}, u32[]{:S(2)}, u32[]{:S(2)}) async-start(f32[8,256,256]{2,1,0:T(8,128)} %copy.46), calls=%async_computation.2 | async-start | bytes 4194304 | tf_op jit(solution)/shard_map/all_to_all | solution.py:77
  144.8 91.4 %all-gather.5.cloned.1.call-start = ((), (), s32[]{:S(2)}) async-start(), calls=%async_computation.4 | async-start | bytes 2359296 | tf_op jit(solution)/shard_map/all_gather | solution.py:91
  196.5 4.2 %copy-start.2 = (f32[1024,256]{1,0:T(8,128)S(1)}, f32[1024,256]{1,0:T(8,128)}, u32[]{:S(2)}) copy-start(f32[1024,256]{1,0:T(8,128)} %get-tuple-element.7) | copy-start | bytes 3145732
Sparse Core Ops, SparseCore 0:
  38.9 92.1 all-gather.2
  148.8 87.3 all-gather.4
where the time goes:
time: 256 us; the launch traced here: 255 us
  waiting for transfers between devices  158 us (62%)
  local copies, waits for them, and re-layouts  27 us (11%)
  starting transfers between devices  26.9 us (11%)
  matrix products  16.3 us (6%)
  between operations  13.6 us (5%)
  other arithmetic  13 us (5%)
    all_to_all x2, waiting for transfers between devices, several_exchanges(): lax.all_to_all(share, axis, split_axis=0, concat_axis=0, tiled=True)  56.6 us
    all_to_all x1, waiting for transfers between devices, body(): lax.all_to_all(sending, 'gy', split_axis=0, concat_axis=0, tiled=True)  50.6 us
    all_gather x1, waiting for transfers between devices, body(): lax.all_gather(parent_inv, 'gz', axis=1, tiled=True)  34.3 us
    all_to_all x2, starting transfers between devices, several_exchanges(): lax.all_to_all(share, axis, split_axis=0, concat_axis=0, tiled=True)  20.9 us
    all_gather x1, waiting for transfers between devices, side_by_side(): lax.all_gather(both, axis, axis=dim, tiled=True)  15.8 us
    gather x1, local copies, waits for them, and re-layouts, body(): front_rows = jnp.take(arrived, recv_order[0], axis=0)  10.2 us
    gather x1, local copies, waits for them, and re-layouts, body(): outgoing = jnp.take(right_side, send_order[0], axis=0)  8.6 us
    dot_general x1, matrix products, body(): jnp.einsum('pij,pjc->pic', lax.all_gather(parent_inv, 'gz', axis=1, tiled...  6.39 us
  transfers between devices with their start and end apart: 5, of which 5 were waited for; matrix products, arithmetic and copies ran while one was open for 9% of the time, Pallas kernels for 0%

commit v1 on v0

v1 whole, which is shorter than its diff:
```python
import functools

import jax
import jax.numpy as jnp
from jax import lax
from jax.experimental import pallas as pl
from jax.experimental.pallas import tpu as pltpu
from jax.sharding import PartitionSpec as P

PIV = 256
BLK = 128
LEAF_DEV = 4
PAR_DEV = 2
OWN = PAR_DEV * 4
NX = 4
MESH = pl.DeviceIdType.MESH
Y_ORDER = (4, 1, 7, 2, 6, 3, 5, 0)
LANES = 128
HIGH = lax.Precision.HIGHEST


def dot(a, b):
    return jnp.dot(a, b, precision=HIGH, preferred_element_type=jnp.float32)


def kernel(
    n_gx, n_gy, n_gz,
    send_order, recv_order, target,
    rhs_hbm, inv_hbm, low_hbm, par_hbm,
    out,
    rhs_a, rhs_b, pack_a, pack_b, got_a, got_b, front_a, front_b,
    inv_all, low_all, par_all, upd, slots_a, slots_b, in_a, in_b,
    load_sem, z_send, z_recv, x_send, x_recv, f_send, f_recv,
    rows_send, rows_recv, upd_send, upd_recv,
):
    gx, gy, gz = lax.axis_index("gx"), lax.axis_index("gy"), lax.axis_index("gz")
    me = gx * n_gy + gy
    places = n_gx * n_gy
    share = rhs_a.shape[0] // places
    z_peer = gz + 1 - 2 * lax.rem(gz, 2)

    halves = (
        (rhs_a, pack_a, got_a, front_a, slots_a, in_a),
        (rhs_b, pack_b, got_b, front_b, slots_b, in_b),
    )
    loads = [
        pltpu.make_async_copy(rhs_hbm.at[:, pl.ds(0, LANES)], rhs_a, load_sem.at[0]),
        pltpu.make_async_copy(inv_hbm, inv_all.at[gz], load_sem.at[1]),
        pltpu.make_async_copy(low_hbm, low_all.at[gz], load_sem.at[2]),
        pltpu.make_async_copy(rhs_hbm.at[:, pl.ds(LANES, LANES)], rhs_b, load_sem.at[3]),
        pltpu.make_async_copy(par_hbm, par_all.at[gz], load_sem.at[4]),
    ]
    for load in loads:
        load.start()

    def place_of(i, j):
        other = lax.bitwise_xor(gx, lax.rem(i + j, n_gx))
        return other, lax.rem(gy + Y_ORDER[j], n_gy), lax.rem(i + j, n_gx)

    barrier = pltpu.get_barrier_semaphore()

    @pl.loop(0, n_gx)
    def _(i):
        for j in range(n_gy):
            px, py, turn = place_of(i, j)
            if Y_ORDER[j] == 0:
                @pl.when(turn != 0)
                def _():
                    pl.semaphore_signal(barrier, inc=1, device_id=(px, py, gz), device_id_type=MESH)
            else:
                pl.semaphore_signal(barrier, inc=1, device_id=(px, py, gz), device_id_type=MESH)

    def x_peer(k):
        return lax.rem(gz + 2 * k, n_gz)

    pl.semaphore_signal(barrier, inc=1, device_id=(gx, gy, z_peer), device_id_type=MESH)
    for k in range(1, NX):
        pl.semaphore_signal(barrier, inc=1, device_id=(gx, gy, x_peer(k)), device_id_type=MESH)

    def gather_rows(source, order, sink):
        @pl.loop(0, sink.shape[0] // share)
        def _(c):
            base = pl.multiple_of(c * share, share)
            for r in range(share):
                sink[pl.ds(base + r, 1), :] = source[pl.ds(order[base + r], 1), :]

    def send_rows(pack, got, h):
        got[pl.ds(pl.multiple_of(me * share, share), share), :] = pack[
            pl.ds(pl.multiple_of(me * share, share), share), :
        ]

        def send(px, py):
            there = px * n_gy + py
            pltpu.make_async_remote_copy(
                src_ref=pack.at[pl.ds(pl.multiple_of(there * share, share), share)],
                dst_ref=got.at[pl.ds(pl.multiple_of(me * share, share), share)],
                send_sem=rows_send.at[h],
                recv_sem=rows_recv.at[h],
                device_id=(px, py, gz),
                device_id_type=MESH,
            ).start()

        @pl.loop(0, n_gx)
        def _(i):
            for j in range(n_gy):
                px, py, turn = place_of(i, j)
                if Y_ORDER[j] == 0:
                    @pl.when(turn != 0)
                    def _():
                        send(px, py)
                else:
                    send(px, py)

    whole = (inv_all, low_all, par_all)

    def z_copy(w):
        return pltpu.make_async_remote_copy(
            src_ref=whole[w].at[gz], dst_ref=whole[w].at[gz],
            send_sem=z_send.at[w], recv_sem=z_recv.at[w],
            device_id=(gx, gy, z_peer), device_id_type=MESH,
        )

    def x_copy(w, k):
        return pltpu.make_async_remote_copy(
            src_ref=whole[w].at[gz], dst_ref=whole[w].at[gz],
            send_sem=x_send.at[w, k - 1], recv_sem=x_recv.at[w, k - 1],
            device_id=(gx, gy, x_peer(k)), device_id_type=MESH,
        )

    def f_copy(w, k):
        return pltpu.make_async_remote_copy(
            src_ref=whole[w].at[z_peer], dst_ref=whole[w].at[z_peer],
            send_sem=f_send.at[w, k - 1], recv_sem=f_recv.at[w, k - 1],
            device_id=(gx, gy, x_peer(k)), device_id_type=MESH,
        )

    def share_factor(w):
        z_copy(w).start()
        for k in (1, 3, 2):
            x_copy(w, k).start()

    def forward_factor(w):
        z_copy(w).wait_recv()
        for k in (1, 3, 2):
            f_copy(w, k).start()

    def await_factor(w):
        for k in range(1, NX):
            x_copy(w, k).wait_recv()
            f_copy(w, k).wait_recv()

    def splat(leaf, j):
        return jnp.full((8, LANES), target[leaf, j], jnp.int32)

    def owned_by(first, place):
        return jnp.logical_and(first >= place * OWN, first < place * OWN + OWN)

    def keep(mask, new, old):
        shape = new.shape
        tiles = (shape[0] // 8, 8, LANES)
        mask = jnp.broadcast_to(mask[None], tiles)
        return jnp.where(mask, new.reshape(tiles), old.reshape(tiles)).reshape(shape)

    def leaf_stage(h):
        got, front, slots, arriving = halves[h][2], halves[h][3], halves[h][4], halves[h][5]
        cols = pl.ds(h * LANES, LANES)
        gather_rows(got, recv_order, front)
        for l in range(LEAF_DEV):
            rows = pl.ds(l * PIV, PIV)
            sol = dot(inv_all[:, l].reshape(PIV, PIV), front[rows, :])
            out[rows, cols] = sol
            upd[h, l] = dot(low_all[:, l].reshape(PIV, PIV), sol)
        firsts = [splat(gy * LEAF_DEV + l, 0) for l in range(LEAF_DEV)]
        for step in Y_ORDER:
            there = lax.rem(gy + step, n_gy)
            masks = [owned_by(firsts[l], there) for l in range(1, LEAF_DEV)]
            for part in range(0, PIV, BLK):
                rows = pl.ds(part, BLK)
                chosen = upd[h, 0, rows, :]
                for l in range(1, LEAF_DEV):
                    chosen = keep(masks[l - 1], upd[h, l, rows, :], chosen)
                if step == 0:
                    arriving[gy, rows, :] = chosen
                else:
                    slots[step, rows, :] = chosen
        for step in Y_ORDER:
            if step:
                there = lax.rem(gy + step, n_gy)
                pltpu.make_async_remote_copy(
                    src_ref=slots.at[step], dst_ref=arriving.at[gy],
                    send_sem=upd_send.at[h], recv_sem=upd_recv.at[h],
                    device_id=(gx, there, gz), device_id_type=MESH,
                ).start()

    def parent_stage(h):
        front, arriving = halves[h][3], halves[h][5]
        cols = pl.ds(h * LANES, LANES)
        zeros = jnp.zeros((BLK, LANES), jnp.float32)
        first, second = [], []
        for s in range(n_gy):
            one = two = jnp.full((8, LANES), -1, jnp.int32)
            for l in range(LEAF_DEV):
                t_one, t_two = splat(s * LEAF_DEV + l, 0), splat(s * LEAF_DEV + l, 1)
                mine = owned_by(t_one, gy)
                one = jnp.where(mine, t_one, one)
                two = jnp.where(mine, t_two, two)
            first.append(one)
            second.append(two)
        for p in range(PAR_DEV):
            for q in range(4):
                b = p * 4 + q
                here = gy * OWN + b
                total = zeros
                for s in range(n_gy):
                    piece = keep(second[s] == here, arriving[s, pl.ds(BLK, BLK), :], zeros)
                    total = total + keep(first[s] == here, arriving[s, pl.ds(0, BLK), :], piece)
                rows = pl.ds(LEAF_DEV * PIV + b * BLK, BLK)
                front[rows, :] = front[rows, :] - total
        for p in range(PAR_DEV):
            rows = pl.ds(LEAF_DEV * PIV + p * 4 * BLK, 4 * BLK)
            out[rows, cols] = dot(par_all[:, p].reshape(4 * BLK, 4 * BLK), front[rows, :])

    def bulk(ref, sem, count):
        part = ref.at[pl.ds(0, count)]
        return pltpu.make_async_copy(part, part, sem)

    others = (places - 1) * share
    loads[0].wait()
    gather_rows(rhs_a, send_order, pack_a)
    loads[1].wait()
    loads[2].wait()
    pl.semaphore_wait(barrier, places - 1 + NX)
    share_factor(0)
    share_factor(1)
    send_rows(pack_a, got_a, 0)
    loads[3].wait()
    gather_rows(rhs_b, send_order, pack_b)
    send_rows(pack_b, got_b, 1)
    loads[4].wait()
    share_factor(2)
    forward_factor(0)
    forward_factor(1)
    bulk(got_a, rows_recv.at[0], others).wait()
    await_factor(0)
    await_factor(1)
    leaf_stage(0)
    forward_factor(2)
    bulk(got_b, rows_recv.at[1], others).wait()
    leaf_stage(1)
    await_factor(2)
    bulk(in_a, upd_recv.at[0], n_gy - 1).wait()
    parent_stage(0)
    bulk(in_b, upd_recv.at[1], n_gy - 1).wait()
    parent_stage(1)
    for w in range(3):
        z_copy(w).wait_send()
        for k in range(1, NX):
            x_copy(w, k).wait_send()
            f_copy(w, k).wait_send()
    for h in range(2):
        bulk(halves[h][1], rows_send.at[h], others).wait()
        bulk(halves[h][4], upd_send.at[h], n_gy - 1).wait()


def body(sizes, right_side, send_order, recv_order, update_target, leaf_inv, leaf_low, parent_inv):
    n_gx, n_gy, n_gz = sizes
    rows = right_side.shape[0]
    f32 = jnp.float32
    any_space = pl.BlockSpec(memory_space=pl.ANY)
    smem = pl.BlockSpec(memory_space=pltpu.SMEM)
    half = pltpu.VMEM((rows, LANES), f32)
    dma = pltpu.SemaphoreType.DMA
    return pl.pallas_call(
        functools.partial(kernel, n_gx, n_gy, n_gz),
        out_shape=jax.ShapeDtypeStruct(right_side.shape, f32),
        in_specs=[smem, smem, smem, any_space, any_space, any_space, any_space],
        out_specs=pl.BlockSpec(memory_space=pltpu.VMEM),
        scratch_shapes=[
            half, half, half, half, half, half, half, half,
            pltpu.VMEM((n_gz,) + leaf_inv.shape, f32),
            pltpu.VMEM((n_gz,) + leaf_low.shape, f32),
            pltpu.VMEM((n_gz,) + parent_inv.shape, f32),
            pltpu.VMEM((2, LEAF_DEV, PIV, LANES), f32),
            pltpu.VMEM((n_gy, PIV, LANES), f32),
            pltpu.VMEM((n_gy, PIV, LANES), f32),
            pltpu.VMEM((n_gy, PIV, LANES), f32),
            pltpu.VMEM((n_gy, PIV, LANES), f32),
            dma((5,)), dma((3,)), dma((3,)),
            dma((3, NX - 1)), dma((3, NX - 1)), dma((3, NX - 1)), dma((3, NX - 1)),
            dma((2,)), dma((2,)), dma((2,)), dma((2,)),
        ],
        compiler_params=pltpu.CompilerParams(
            collective_id=0, has_side_effects=True, vmem_limit_bytes=56 * 2**20
        ),
        name="forward_solve",
    )(
        send_order.reshape(-1), recv_order.reshape(-1), update_target,
        right_side, leaf_inv, leaf_low, parent_inv,
    )


def solution(mesh):
    sizes = (mesh.shape["gx"], mesh.shape["gy"], mesh.shape["gz"])
    placed = (
        P(("gx", "gy"), "gz"),
        P(("gx", "gy"), None),
        P(("gx", "gy"), None),
        P("gx", None),
        P(("gx", "gy"), "gz", None),
        P(("gx", "gy"), "gz", None),
        P(("gx", "gy"), "gz", None),
    )
    return jax.shard_map(
        functools.partial(body, sizes), mesh=mesh, in_specs=placed,
        out_specs=P(("gx", "gy"), "gz"), check_vma=False,
    )
```

time: 256 us -> 146 us (0.57)
  waiting for transfers between devices: 158 us -> 0 us
  Pallas kernels: 0 us -> 139 us
  starting transfers between devices: 26.9 us -> 0 us
  local copies, waits for them, and re-layouts: 27 us -> 4.41 us
  matrix products: 16.3 us -> 0 us
  between operations: 13.6 us -> 0.01 us
  other arithmetic: 13 us -> 0 us
    pallas_call x0 -> x1, Pallas kernels: none -> 139 us  [body(): pl.pallas_call(functools.partial(kernel, n_gx, n_gy, n_gz), out_shape=jax...]
    all_to_all x3 -> x0, waiting for transfers between devices: 107 us -> none  [the longest x2 56.6 us: several_exchanges(): lax.all_to_all(share, axis, split_axis=0, concat_axis=0, tiled=True)]
    all_gather x2 -> x0, waiting for transfers between devices: 50.2 us -> none  [the longest x1 34.3 us: body(): lax.all_gather(parent_inv, 'gz', axis=1, tiled=True)]
    all_to_all x3 -> x0, starting transfers between devices: 26.6 us -> none  [the longest x2 20.9 us: several_exchanges(): lax.all_to_all(share, axis, split_axis=0, concat_axis=0, tiled=True)]
    gather x2 -> x0, local copies, waits for them, and re-layouts: 18.8 us -> none  [the longest x1 10.2 us: body(): front_rows = jnp.take(arrived, recv_order[0], axis=0)]
    dot_general x6 -> x0, matrix products: 16.3 us -> none  [the longest x1 6.39 us: body(): jnp.einsum('pij,pjc->pic', lax.all_gather(parent_inv, 'gz', axis=1, tiled...]
    concatenate x3 -> x0, other arithmetic: 6.18 us -> none  [the longest x1 2.76 us: several_exchanges(): return in_order(jnp.concatenate(finished, axis=split_at), concat_dim)]
    dot_general x3 -> x0, local copies, waits for them, and re-layouts: 4.84 us -> none  [the longest x1 2.53 us: body(): jnp.einsum('pij,pjc->pic', lax.all_gather(parent_inv, 'gz', axis=1, tiled...]
  transfers between devices with their start and end apart: 5 -> 0, of which waited for: 5 -> 0; matrix products, arithmetic and copies ran while one was open for 9% -> 0% of each run, Pallas kernels for 0% -> 0%
where the time goes in v1:
time: 146 us; the launch traced here: 143 us
  Pallas kernels  139 us (95%)
  local copies, waits for them, and re-layouts  4.41 us (3%)
    pallas_call x1, Pallas kernels, body(): pl.pallas_call(functools.partial(kernel, n_gx, n_gy, n_gz), out_shape=jax...  139 us
    unnamed x2, local copies, waits for them, and re-layouts  4.41 us

profile of v1, /device:TPU:1, one launch (start us, length us, event | category | flops | bytes accessed | tf_op | source)
XLA Modules:
  0.0 143.1 jit_solution(11553295421932733300)
XLA Ops:
  0.0 1.4 copy.8.target
  1.4 138.6 %forward_solve.1 = f32[2048,256]{1,0:T(8,128)} custom-call(s32[2048]{0:T(1024)} %bitcast.2, s32[2048]{0:T(1024)} %bitcast.3, s32[32,2]{1,0:T(8,128)} %copy.8.target, f32[2048,256]{1,0:T(8,128)} %rhs_hbm.1, f32[4,32,256]{2,1,0:T(8,128)} %inv_hbm.1, f32[4,32,256]{2,1,0:T(8,128)} %low_hbm.1, f32[2,64,512]{2,1,0:T(8,128)} %par_hbm.1), custom_call_target="tpu_custom_call" | custom-call | tf_op jit(solution)/shard_map/forward_solve/pallas_call | solution.py:273
  140.0 3.0 %copy.10 = f32[2048,256]{1,0:T(8,128)} copy(f32[2048,256]{1,0:T(8,128)} %forward_solve.1) | data formatting | bytes 4194304

commit v2 on v1

v2 whole, which is shorter than its diff:
```python
import functools

import jax
import jax.numpy as jnp
from jax import lax
from jax.experimental import pallas as pl
from jax.experimental.pallas import tpu as pltpu
from jax.sharding import PartitionSpec as P

PIV = 256
BLK = 128
LEAF_DEV = 4
PAR_DEV = 2
OWN = PAR_DEV * 4
NX = 4
MESH = pl.DeviceIdType.MESH
Y_ORDER = (4, 3, 5, 2, 6, 1, 7)
G_FAR = (6, 7, 4, 5)
G_NEAR = (2, 3, 1)
LANES = 128
HIGH = lax.Precision.HIGHEST


def dot(a, b):
    return jnp.dot(a, b, precision=HIGH, preferred_element_type=jnp.float32)


def kernel(
    n_gx, n_gy, n_gz,
    send_order, recv_order, target,
    rhs_hbm, inv_hbm, low_hbm, par_hbm,
    out,
    rhs_a, rhs_b, pack_a, pack_b, mid_a, mid_b, got_a, got_b, front_a, front_b,
    inv_all, low_all, par_all, upd, slots_a, slots_b, in_a, in_b,
    load_sem, z_send, z_recv, x_send, x_recv, f_send, f_recv,
    y_send, y_recv, g_send, g_recv, upd_send, upd_recv,
):
    gx, gy, gz = lax.axis_index("gx"), lax.axis_index("gy"), lax.axis_index("gz")
    part = n_gx // 2
    share = rhs_a.shape[0] // (n_gx * n_gy)
    lot = n_gy * share
    z_peer = gz + 1 - 2 * lax.rem(gz, 2)
    near = gx // part
    far = 1 - near

    rhs, pack, mid = (rhs_a, rhs_b), (pack_a, pack_b), (mid_a, mid_b)
    got, front = (got_a, got_b), (front_a, front_b)
    slots, arrived = (slots_a, slots_b), (in_a, in_b)
    loads = [
        pltpu.make_async_copy(rhs_hbm.at[:, pl.ds(0, LANES)], rhs_a, load_sem.at[0]),
        pltpu.make_async_copy(inv_hbm, inv_all.at[gz], load_sem.at[1]),
        pltpu.make_async_copy(low_hbm, low_all.at[gz], load_sem.at[2]),
        pltpu.make_async_copy(rhs_hbm.at[:, pl.ds(LANES, LANES)], rhs_b, load_sem.at[3]),
        pltpu.make_async_copy(par_hbm, par_all.at[gz], load_sem.at[4]),
    ]
    for load in loads:
        load.start()

    barrier = pltpu.get_barrier_semaphore()

    def greet(px, py, pz):
        pl.semaphore_signal(barrier, inc=1, device_id=(px, py, pz), device_id_type=MESH)

    def x_peer(k):
        return lax.rem(gz + 2 * k, n_gz)

    for step in Y_ORDER:
        greet(gx, lax.rem(gy + step, n_gy), gz)
    for turn in G_FAR + G_NEAR:
        greet(lax.bitwise_xor(gx, turn), gy, gz)
    greet(gx, gy, z_peer)
    for k in range(1, NX):
        greet(gx, gy, x_peer(k))

    def pick_rows(h, side):
        @pl.loop(0, part)
        def _(i):
            for y in range(n_gy):
                place = (side * part + i) * n_gy + y
                base = place * share

                @pl.loop(0, share // 8)
                def _(t):
                    for r in range(8):
                        at = t * 8 + r
                        pack[h][side * part + i, pl.ds(y * share + at, 1), :] = rhs[h][
                            pl.ds(send_order[base + at], 1), :
                        ]

    def send_along_y(h, side, far_or_near):
        places = pl.ds(pl.multiple_of(side * part, part), part)
        own = pl.ds(pl.multiple_of(gy * share, share), share)
        for step in Y_ORDER:
            there = lax.rem(gy + step, n_gy)
            pltpu.make_async_remote_copy(
                src_ref=pack[h].at[places, pl.ds(pl.multiple_of(there * share, share), share)],
                dst_ref=mid[h].at[places, own],
                send_sem=y_send.at[h],
                recv_sem=y_recv.at[h, far_or_near],
                device_id=(gx, there, gz),
                device_id_type=MESH,
            ).start()
        mid[h][places, own, :] = pack[h][places, own, :]

    def await_y(h, far_or_near):
        bulk(mid[h].at[pl.ds(0, part), pl.ds(0, (n_gy - 1) * share)], y_recv.at[h, far_or_near])

    def send_along_gx(h, turns, far_or_near):
        own = pl.ds(pl.multiple_of(gx * lot, lot), lot)
        for turn in turns:
            there = lax.bitwise_xor(gx, turn)
            pltpu.make_async_remote_copy(
                src_ref=mid[h].at[there],
                dst_ref=got[h].at[own],
                send_sem=g_send.at[h],
                recv_sem=g_recv.at[h, far_or_near],
                device_id=(there, gy, gz),
                device_id_type=MESH,
            ).start()

    def keep_own(h):
        got[h][pl.ds(pl.multiple_of(gx * lot, lot), lot), :] = mid[h][gx]

    def await_gx(h):
        bulk(got[h].at[pl.ds(0, len(G_FAR) * lot)], g_recv.at[h, 0])
        bulk(got[h].at[pl.ds(0, len(G_NEAR) * lot)], g_recv.at[h, 1])

    def bulk(view, sem):
        pltpu.make_async_copy(view, view, sem).wait()

    def take_rows(h):
        @pl.loop(0, front[h].shape[0] // 32)
        def _(c):
            base = pl.multiple_of(c * 32, 32)
            for r in range(32):
                front[h][pl.ds(base + r, 1), :] = got[h][pl.ds(recv_order[base + r], 1), :]

    whole = (inv_all, low_all, par_all)

    def z_copy(w):
        return pltpu.make_async_remote_copy(
            src_ref=whole[w].at[gz], dst_ref=whole[w].at[gz],
            send_sem=z_send.at[w], recv_sem=z_recv.at[w],
            device_id=(gx, gy, z_peer), device_id_type=MESH,
        )

    def x_copy(w, k):
        return pltpu.make_async_remote_copy(
            src_ref=whole[w].at[gz], dst_ref=whole[w].at[gz],
            send_sem=x_send.at[w, k - 1], recv_sem=x_recv.at[w, k - 1],
            device_id=(gx, gy, x_peer(k)), device_id_type=MESH,
        )

    def f_copy(w, k):
        return pltpu.make_async_remote_copy(
            src_ref=whole[w].at[z_peer], dst_ref=whole[w].at[z_peer],
            send_sem=f_send.at[w, k - 1], recv_sem=f_recv.at[w, k - 1],
            device_id=(gx, gy, x_peer(k)), device_id_type=MESH,
        )

    def share_along_x(w):
        for k in (1, 3, 2):
            x_copy(w, k).start()

    def forward_factor(w):
        z_copy(w).wait_recv()
        for k in (1, 3, 2):
            f_copy(w, k).start()

    def await_factor(w):
        for k in range(1, NX):
            x_copy(w, k).wait_recv()
            f_copy(w, k).wait_recv()

    def splat(leaf, j):
        return jnp.full((8, LANES), target[j, leaf], jnp.int32)

    def owned_by(first, place):
        return jnp.logical_and(first >= place * OWN, first < place * OWN + OWN)

    def keep(mask, new, old):
        shape = new.shape
        tiles = (shape[0] // 8, 8, LANES)
        mask = jnp.broadcast_to(mask[None], tiles)
        return jnp.where(mask, new.reshape(tiles), old.reshape(tiles)).reshape(shape)

    def leaf_stage(h):
        cols = pl.ds(h * LANES, LANES)
        take_rows(h)
        for l in range(LEAF_DEV):
            rows = pl.ds(l * PIV, PIV)
            sol = dot(inv_all[:, l].reshape(PIV, PIV), front[h][rows, :])
            out[rows, cols] = sol
            upd[h, l] = dot(low_all[:, l].reshape(PIV, PIV), sol)
        firsts = [splat(gy * LEAF_DEV + l, 0) for l in range(LEAF_DEV)]
        for step in Y_ORDER + (0,):
            there = lax.rem(gy + step, n_gy)
            masks = [owned_by(firsts[l], there) for l in range(1, LEAF_DEV)]
            for part in range(0, PIV, BLK):
                rows = pl.ds(part, BLK)
                chosen = upd[h, 0, rows, :]
                for l in range(1, LEAF_DEV):
                    chosen = keep(masks[l - 1], upd[h, l, rows, :], chosen)
                if step == 0:
                    arrived[h][gy, rows, :] = chosen
                else:
                    slots[h][step, rows, :] = chosen
        for step in Y_ORDER:
            pltpu.make_async_remote_copy(
                src_ref=slots[h].at[step], dst_ref=arrived[h].at[gy],
                send_sem=upd_send.at[h], recv_sem=upd_recv.at[h],
                device_id=(gx, lax.rem(gy + step, n_gy), gz), device_id_type=MESH,
            ).start()

    def parent_stage(h):
        cols = pl.ds(h * LANES, LANES)
        zeros = jnp.zeros((BLK, LANES), jnp.float32)
        first, second = [], []
        for s in range(n_gy):
            one = two = jnp.full((8, LANES), -1, jnp.int32)
            for l in range(LEAF_DEV):
                t_one, t_two = splat(s * LEAF_DEV + l, 0), splat(s * LEAF_DEV + l, 1)
                mine = owned_by(t_one, gy)
                one = jnp.where(mine, t_one, one)
                two = jnp.where(mine, t_two, two)
            first.append(one)
            second.append(two)
        for p in range(PAR_DEV):
            for q in range(4):
                b = p * 4 + q
                here = gy * OWN + b
                total = zeros
                for s in range(n_gy):
                    piece = keep(second[s] == here, arrived[h][s, pl.ds(BLK, BLK), :], zeros)
                    total = total + keep(first[s] == here, arrived[h][s, pl.ds(0, BLK), :], piece)
                rows = pl.ds(LEAF_DEV * PIV + b * BLK, BLK)
                front[h][rows, :] = front[h][rows, :] - total
        for p in range(PAR_DEV):
            rows = pl.ds(LEAF_DEV * PIV + p * 4 * BLK, 4 * BLK)
            out[rows, cols] = dot(par_all[:, p].reshape(4 * BLK, 4 * BLK), front[h][rows, :])

    loads[0].wait()
    pick_rows(0, far)
    loads[1].wait()
    loads[2].wait()
    pl.semaphore_wait(barrier, n_gx + n_gy - 2 + NX)
    z_copy(0).start()
    z_copy(1).start()
    send_along_y(0, far, 0)
    share_along_x(0)
    share_along_x(1)
    pick_rows(0, near)
    send_along_y(0, near, 1)
    loads[3].wait()
    pick_rows(1, far)
    pick_rows(1, near)
    loads[4].wait()
    share_along_x(2)
    await_y(0, 0)
    send_along_gx(0, G_FAR, 0)
    send_along_y(1, far, 0)
    forward_factor(0)
    forward_factor(1)
    await_y(0, 1)
    send_along_gx(0, G_NEAR, 1)
    send_along_y(1, near, 1)
    keep_own(0)
    await_gx(0)
    await_y(1, 0)
    send_along_gx(1, G_FAR, 0)
    await_factor(0)
    await_factor(1)
    leaf_stage(0)
    await_y(1, 1)
    send_along_gx(1, G_NEAR, 1)
    keep_own(1)
    await_gx(1)
    z_copy(2).start()
    leaf_stage(1)
    forward_factor(2)
    await_factor(2)
    bulk(in_a.at[pl.ds(0, n_gy - 1)], upd_recv.at[0])
    parent_stage(0)
    bulk(in_b.at[pl.ds(0, n_gy - 1)], upd_recv.at[1])
    parent_stage(1)
    for w in range(3):
        z_copy(w).wait_send()
        for k in range(1, NX):
            x_copy(w, k).wait_send()
            f_copy(w, k).wait_send()
    for h in range(2):
        bulk(mid[h].at[:, pl.ds(0, (n_gy - 1) * share)], y_send.at[h])
        bulk(got[h].at[pl.ds(0, (n_gx - 1) * lot)], g_send.at[h])
        bulk(slots[h].at[pl.ds(0, n_gy - 1)], upd_send.at[h])


def body(sizes, right_side, send_order, recv_order, update_target, leaf_inv, leaf_low, parent_inv):
    n_gx, n_gy, n_gz = sizes
    rows = right_side.shape[0]
    f32 = jnp.float32
    any_space = pl.BlockSpec(memory_space=pl.ANY)
    smem = pl.BlockSpec(memory_space=pltpu.SMEM)
    half = pltpu.VMEM((rows, LANES), f32)
    lots = pltpu.VMEM((n_gx, rows // n_gx, LANES), f32)
    dma = pltpu.SemaphoreType.DMA
    return pl.pallas_call(
        functools.partial(kernel, n_gx, n_gy, n_gz),
        out_shape=pltpu.VMEM(right_side.shape, f32),
        in_specs=[smem, smem, smem, any_space, any_space, any_space, any_space],
        out_specs=pl.BlockSpec(memory_space=pltpu.VMEM),
        scratch_shapes=[
            half, half, lots, lots, lots, lots, half, half, half, half,
            pltpu.VMEM((n_gz,) + leaf_inv.shape, f32),
            pltpu.VMEM((n_gz,) + leaf_low.shape, f32),
            pltpu.VMEM((n_gz,) + parent_inv.shape, f32),
            pltpu.VMEM((2, LEAF_DEV, PIV, LANES), f32),
            pltpu.VMEM((n_gy, PIV, LANES), f32),
            pltpu.VMEM((n_gy, PIV, LANES), f32),
            pltpu.VMEM((n_gy, PIV, LANES), f32),
            pltpu.VMEM((n_gy, PIV, LANES), f32),
            dma((5,)), dma((3,)), dma((3,)),
            dma((3, NX - 1)), dma((3, NX - 1)), dma((3, NX - 1)), dma((3, NX - 1)),
            dma((2,)), dma((2, 2)), dma((2,)), dma((2, 2)), dma((2,)), dma((2,)),
        ],
        compiler_params=pltpu.CompilerParams(
            collective_id=0, has_side_effects=True, vmem_limit_bytes=61 * 2**20 + 7 * 2**17
        ),
        name="forward_solve",
    )(
        send_order.reshape(-1), recv_order.reshape(-1), update_target.T,
        right_side, leaf_inv, leaf_low, parent_inv,
    )


def solution(mesh):
    sizes = (mesh.shape["gx"], mesh.shape["gy"], mesh.shape["gz"])
    placed = (
        P(("gx", "gy"), "gz"),
        P(("gx", "gy"), None),
        P(("gx", "gy"), None),
        P("gx", None),
        P(("gx", "gy"), "gz", None),
        P(("gx", "gy"), "gz", None),
        P(("gx", "gy"), "gz", None),
    )
    return jax.shard_map(
        functools.partial(body, sizes), mesh=mesh, in_specs=placed,
        out_specs=P(("gx", "gy"), "gz"), check_vma=False,
    )
```

time: 146 us -> 113 us (0.77); the launches traced: 143 us -> 113 us
  Pallas kernels: 139 us -> 111 us
  local copies, waits for them, and re-layouts: 4.41 us -> 1.32 us
    pallas_call x1, Pallas kernels: 139 us -> 111 us  [body(): pl.pallas_call(functools.partial(kernel, n_gx, n_gy, n_gz), out_shape=plt...]
    unnamed x2 -> x1, local copies, waits for them, and re-layouts: 4.41 us -> 1.32 us
where the time goes in v2:
time: 113 us
  Pallas kernels  111 us (98%)
  local copies, waits for them, and re-layouts  1.32 us (1%)
    pallas_call x1, Pallas kernels, body(): pl.pallas_call(functools.partial(kernel, n_gx, n_gy, n_gz), out_shape=plt...  111 us

profile of v2, /device:TPU:1, one launch (start us, length us, event | category | flops | bytes accessed | tf_op | source)
XLA Modules:
  0.0 112.6 jit_solution(8443907041448974841)
XLA Ops:
  0.0 111.2 %forward_solve.1 = f32[2048,256]{1,0:T(8,128)S(1)} custom-call(s32[2048]{0:T(1024)} %bitcast.3, s32[2048]{0:T(1024)} %bitcast.4, s32[2,32]{1,0:T(2,128)} %bitcast.5, f32[2048,256]{1,0:T(8,128)} %rhs_hbm.1, f32[4,32,256]{2,1,0:T(8,128)} %inv_hbm.1, f32[4,32,256]{2,1,0:T(8,128)} %low_hbm.1, f32[2,64,512]{2,1,0:T(8,128)} %par_hbm.1), custom_call_target="tpu_custom_call" | custom-call | tf_op jit(solution)/shard_map/forward_solve/pallas_call | solution.py:306
  111.2 1.3 %copy.9 = f32[2048,256]{1,0:T(8,128)} copy(f32[2048,256]{1,0:T(8,128)S(1)} %forward_solve.1) | data formatting | bytes 4194304

commit v3 on v2

--- a/solution.py
+++ b/solution.py
@@ -27,11 +27,12 @@
 
 def kernel(
     n_gx, n_gy, n_gz,
-    send_order, recv_order, target,
+    send_hbm, recv_hbm, target_hbm,
     rhs_hbm, inv_hbm, low_hbm, par_hbm,
     out,
     rhs_a, rhs_b, pack_a, pack_b, mid_a, mid_b, got_a, got_b, front_a, front_b,
     inv_all, low_all, par_all, upd, slots_a, slots_b, in_a, in_b,
+    par_hi, par_lo, send_order, recv_order, target,
     load_sem, z_send, z_recv, x_send, x_recv, f_send, f_recv,
     y_send, y_recv, g_send, g_recv, upd_send, upd_recv,
 ):
@@ -52,9 +53,12 @@
         pltpu.make_async_copy(low_hbm, low_all.at[gz], load_sem.at[2]),
         pltpu.make_async_copy(rhs_hbm.at[:, pl.ds(LANES, LANES)], rhs_b, load_sem.at[3]),
         pltpu.make_async_copy(par_hbm, par_all.at[gz], load_sem.at[4]),
+        pltpu.make_async_copy(send_hbm, send_order, load_sem.at[5]),
+        pltpu.make_async_copy(recv_hbm, recv_order, load_sem.at[6]),
+        pltpu.make_async_copy(target_hbm, target, load_sem.at[7]),
     ]
-    for load in loads:
-        load.start()
+    for n in (5, 0, 1, 2, 4, 3, 6, 7):
+        loads[n].start()
 
     barrier = pltpu.get_barrier_semaphore()
 
@@ -72,20 +76,48 @@
     for k in range(1, NX):
         greet(gx, gy, x_peer(k))
 
+    def turn_of(j):
+        away = (j + 1) // 2
+        return n_gy // 2 + away * (1 - 2 * lax.rem(j, 2))
+
+    def pick_and_send_along_y(h, side, far_or_near):
+        places = pl.ds(pl.multiple_of(side * part, part), part)
+        own = pl.ds(pl.multiple_of(gy * share, share), share)
+
+        @pl.loop(0, n_gy)
+        def _(j):
+            there = lax.rem(gy + turn_of(j), n_gy)
+
+            @pl.loop(0, part)
+            def _(i):
+                place = side * part + i
+                base = (place * n_gy + there) * share
+                at = pl.multiple_of(there * share, share)
+                for r in range(share):
+                    pack[h][place, pl.ds(at + r, 1), :] = rhs[h][pl.ds(send_order[base + r], 1), :]
+
+            @pl.when(j > 0)
+            def _():
+                ready = lax.rem(gy + turn_of(j - 1), n_gy)
+                pltpu.make_async_remote_copy(
+                    src_ref=pack[h].at[places, pl.ds(pl.multiple_of(ready * share, share), share)],
+                    dst_ref=mid[h].at[places, own],
+                    send_sem=y_send.at[h],
+                    recv_sem=y_recv.at[h, far_or_near],
+                    device_id=(gx, ready, gz),
+                    device_id_type=MESH,
+                ).start()
+
+        mid[h][places, own, :] = pack[h][places, own, :]
+
     def pick_rows(h, side):
-        @pl.loop(0, part)
-        def _(i):
-            for y in range(n_gy):
-                place = (side * part + i) * n_gy + y
-                base = place * share
-
-                @pl.loop(0, share // 8)
-                def _(t):
-                    for r in range(8):
-                        at = t * 8 + r
-                        pack[h][side * part + i, pl.ds(y * share + at, 1), :] = rhs[h][
-                            pl.ds(send_order[base + at], 1), :
-                        ]
+        @pl.loop(0, part * n_gy)
+        def _(c):
+            place = side * part + c // n_gy
+            at = pl.multiple_of(lax.rem(c, n_gy) * share, share)
+            base = place * lot + at
+            for r in range(share):
+                pack[h][place, pl.ds(at + r, 1), :] = rhs[h][pl.ds(send_order[base + r], 1), :]
 
     def send_along_y(h, side, far_or_near):
         places = pl.ds(pl.multiple_of(side * part, part), part)
@@ -208,54 +240,78 @@
         for step in Y_ORDER:
             pltpu.make_async_remote_copy(
                 src_ref=slots[h].at[step], dst_ref=arrived[h].at[gy],
-                send_sem=upd_send.at[h], recv_sem=upd_recv.at[h],
+                send_sem=upd_send.at[h], recv_sem=upd_recv.at[h, step],
                 device_id=(gx, lax.rem(gy + step, n_gy), gz), device_id_type=MESH,
             ).start()
 
+    def absorb(h, source):
+        zeros = jnp.zeros((BLK, LANES), jnp.float32)
+        one = two = jnp.full((8, LANES), -1, jnp.int32)
+        for l in range(LEAF_DEV):
+            leaf = source * LEAF_DEV + l
+            t_one, t_two = splat(leaf, 0), splat(leaf, 1)
+            mine = owned_by(t_one, gy)
+            one = jnp.where(mine, t_one, one)
+            two = jnp.where(mine, t_two, two)
+        for b in range(OWN):
+            here = gy * OWN + b
+            rows = pl.ds(LEAF_DEV * PIV + b * BLK, BLK)
+            piece = keep(two == here, arrived[h][source, pl.ds(BLK, BLK), :], zeros)
+            piece = keep(one == here, arrived[h][source, pl.ds(0, BLK), :], piece)
+            front[h][rows, :] = front[h][rows, :] - piece
+
+    def absorb_all(h):
+        absorb(h, gy)
+
+        @pl.loop(0, n_gy - 1)
+        def _(j):
+            turn = turn_of(j)
+            source = lax.rem(gy + n_gy - turn, n_gy)
+            pltpu.make_async_copy(
+                arrived[h].at[source], arrived[h].at[source], upd_recv.at[h, turn]
+            ).wait()
+            absorb(h, source)
+
+    def split(x):
+        high = x.astype(jnp.bfloat16)
+        return high, (x - high.astype(jnp.float32)).astype(jnp.bfloat16)
+
+    def split_parents():
+        for p in range(PAR_DEV):
+            rows = par_all.shape[2]
+            for g in range(n_gz):
+                at = pl.ds(g * rows, rows)
+                par_hi[p, at, :], par_lo[p, at, :] = split(par_all[g, p])
+
     def parent_stage(h):
+        absorb_all(h)
         cols = pl.ds(h * LANES, LANES)
-        zeros = jnp.zeros((BLK, LANES), jnp.float32)
-        first, second = [], []
-        for s in range(n_gy):
-            one = two = jnp.full((8, LANES), -1, jnp.int32)
-            for l in range(LEAF_DEV):
-                t_one, t_two = splat(s * LEAF_DEV + l, 0), splat(s * LEAF_DEV + l, 1)
-                mine = owned_by(t_one, gy)
-                one = jnp.where(mine, t_one, one)
-                two = jnp.where(mine, t_two, two)
-            first.append(one)
-            second.append(two)
-        for p in range(PAR_DEV):
-            for q in range(4):
-                b = p * 4 + q
-                here = gy * OWN + b
-                total = zeros
-                for s in range(n_gy):
-                    piece = keep(second[s] == here, arrived[h][s, pl.ds(BLK, BLK), :], zeros)
-                    total = total + keep(first[s] == here, arrived[h][s, pl.ds(0, BLK), :], piece)
-                rows = pl.ds(LEAF_DEV * PIV + b * BLK, BLK)
-                front[h][rows, :] = front[h][rows, :] - total
         for p in range(PAR_DEV):
             rows = pl.ds(LEAF_DEV * PIV + p * 4 * BLK, 4 * BLK)
-            out[rows, cols] = dot(par_all[:, p].reshape(4 * BLK, 4 * BLK), front[h][rows, :])
-
-    loads[0].wait()
-    pick_rows(0, far)
+            high, low = split(front[h][rows, :])
+            both = jnp.dot(
+                par_hi[p], jnp.concatenate([high, low], axis=1), preferred_element_type=jnp.float32
+            )
+            rest = jnp.dot(par_lo[p], high, preferred_element_type=jnp.float32)
+            out[rows, cols] = both[:, :LANES] + both[:, LANES:] + rest
+
     loads[1].wait()
     loads[2].wait()
+    loads[4].wait()
+    loads[5].wait()
+    loads[0].wait()
     pl.semaphore_wait(barrier, n_gx + n_gy - 2 + NX)
     z_copy(0).start()
     z_copy(1).start()
-    send_along_y(0, far, 0)
-    share_along_x(0)
-    share_along_x(1)
-    pick_rows(0, near)
-    send_along_y(0, near, 1)
+    pick_and_send_along_y(0, far, 0)
+    for w in range(3):
+        share_along_x(w)
+    pick_and_send_along_y(0, near, 1)
     loads[3].wait()
     pick_rows(1, far)
     pick_rows(1, near)
-    loads[4].wait()
-    share_along_x(2)
+    loads[6].wait()
+    loads[7].wait()
     await_y(0, 0)
     send_along_gx(0, G_FAR, 0)
     send_along_y(1, far, 0)
@@ -279,9 +335,8 @@
     leaf_stage(1)
     forward_factor(2)
     await_factor(2)
-    bulk(in_a.at[pl.ds(0, n_gy - 1)], upd_recv.at[0])
+    split_parents()
     parent_stage(0)
-    bulk(in_b.at[pl.ds(0, n_gy - 1)], upd_recv.at[1])
     parent_stage(1)
     for w in range(3):
         z_copy(w).wait_send()
@@ -299,14 +354,13 @@
     rows = right_side.shape[0]
     f32 = jnp.float32
     any_space = pl.BlockSpec(memory_space=pl.ANY)
-    smem = pl.BlockSpec(memory_space=pltpu.SMEM)
     half = pltpu.VMEM((rows, LANES), f32)
     lots = pltpu.VMEM((n_gx, rows // n_gx, LANES), f32)
     dma = pltpu.SemaphoreType.DMA
     return pl.pallas_call(
         functools.partial(kernel, n_gx, n_gy, n_gz),
         out_shape=pltpu.VMEM(right_side.shape, f32),
-        in_specs=[smem, smem, smem, any_space, any_space, any_space, any_space],
+        in_specs=[any_space, any_space, any_space, any_space, any_space, any_space, any_space],
         out_specs=pl.BlockSpec(memory_space=pltpu.VMEM),
         scratch_shapes=[
             half, half, lots, lots, lots, lots, half, half, half, half,
@@ -318,9 +372,14 @@
             pltpu.VMEM((n_gy, PIV, LANES), f32),
             pltpu.VMEM((n_gy, PIV, LANES), f32),
             pltpu.VMEM((n_gy, PIV, LANES), f32),
-            dma((5,)), dma((3,)), dma((3,)),
+            pltpu.VMEM((PAR_DEV, 4 * BLK, 4 * BLK), jnp.bfloat16),
+            pltpu.VMEM((PAR_DEV, 4 * BLK, 4 * BLK), jnp.bfloat16),
+            pltpu.SMEM((rows,), jnp.int32),
+            pltpu.SMEM((rows,), jnp.int32),
+            pltpu.SMEM(update_target.shape[::-1], jnp.int32),
+            dma((8,)), dma((3,)), dma((3,)),
             dma((3, NX - 1)), dma((3, NX - 1)), dma((3, NX - 1)), dma((3, NX - 1)),
-            dma((2,)), dma((2, 2)), dma((2,)), dma((2, 2)), dma((2,)), dma((2,)),
+            dma((2,)), dma((2, 2)), dma((2,)), dma((2, 2)), dma((2,)), dma((2, n_gy)),
         ],
         compiler_params=pltpu.CompilerParams(
             collective_id=0, has_side_effects=True, vmem_limit_bytes=61 * 2**20 + 7 * 2**17

time: 113 us -> 110 us (0.973)
  Pallas kernels: 111 us -> 108 us
    pallas_call x1, Pallas kernels: 111 us -> 108 us  [body(): pl.pallas_call(functools.partial(kernel, n_gx, n_gy, n_gz), out_shape=plt...]
where the time goes in v3:
time: 110 us
  Pallas kernels  108 us (98%)
  local copies, waits for them, and re-layouts  1.32 us (1%)
    pallas_call x1, Pallas kernels, body(): pl.pallas_call(functools.partial(kernel, n_gx, n_gy, n_gz), out_shape=plt...  108 us

profile of v3, /device:TPU:1, one launch (start us, length us, event | category | flops | bytes accessed | tf_op | source)
XLA Modules:
  0.0 109.7 jit_solution(4222582086328550229)
XLA Ops:
  0.0 108.4 %forward_solve.1 = f32[2048,256]{1,0:T(8,128)S(1)} custom-call(s32[2048]{0:T(1024)} %bitcast.3, s32[2048]{0:T(1024)} %bitcast.4, s32[2,32]{1,0:T(2,128)} %bitcast.5, f32[2048,256]{1,0:T(8,128)} %rhs_hbm.1, f32[4,32,256]{2,1,0:T(8,128)} %inv_hbm.1, f32[4,32,256]{2,1,0:T(8,128)} %low_hbm.1, f32[2,64,512]{2,1,0:T(8,128)} %par_hbm.1), custom_call_target="tpu_custom_call" | custom-call | tf_op jit(solution)/shard_map/forward_solve/pallas_call | solution.py:360
  108.4 1.3 %copy.9 = f32[2048,256]{1,0:T(8,128)} copy(f32[2048,256]{1,0:T(8,128)S(1)} %forward_solve.1) | data formatting | bytes 4194304

commit v4 on v3

--- a/solution.py
+++ b/solution.py
@@ -15,14 +15,9 @@
 NX = 4
 MESH = pl.DeviceIdType.MESH
 Y_ORDER = (4, 3, 5, 2, 6, 1, 7)
-G_FAR = (6, 7, 4, 5)
+G_FAR = (4, 5, 6, 7)
 G_NEAR = (2, 3, 1)
 LANES = 128
-HIGH = lax.Precision.HIGHEST
-
-
-def dot(a, b):
-    return jnp.dot(a, b, precision=HIGH, preferred_element_type=jnp.float32)
 
 
 def kernel(
@@ -32,7 +27,7 @@
     out,
     rhs_a, rhs_b, pack_a, pack_b, mid_a, mid_b, got_a, got_b, front_a, front_b,
     inv_all, low_all, par_all, upd, slots_a, slots_b, in_a, in_b,
-    par_hi, par_lo, send_order, recv_order, target,
+    inv_hi, inv_lo, low_hi, low_lo, par_hi, par_lo, send_order, recv_order, target,
     load_sem, z_send, z_recv, x_send, x_recv, f_send, f_recv,
     y_send, y_recv, g_send, g_recv, upd_send, upd_recv,
 ):
@@ -47,6 +42,22 @@
     rhs, pack, mid = (rhs_a, rhs_b), (pack_a, pack_b), (mid_a, mid_b)
     got, front = (got_a, got_b), (front_a, front_b)
     slots, arrived = (slots_a, slots_b), (in_a, in_b)
+    barrier = pltpu.get_barrier_semaphore()
+
+    def greet(px, py, pz):
+        pl.semaphore_signal(barrier, inc=1, device_id=(px, py, pz), device_id_type=MESH)
+
+    def x_peer(k):
+        return lax.rem(gz + 2 * k, n_gz)
+
+    greet(gx, gy, z_peer)
+    for step in Y_ORDER:
+        greet(gx, lax.rem(gy + step, n_gy), gz)
+    for turn in G_FAR + G_NEAR:
+        greet(lax.bitwise_xor(gx, turn), gy, gz)
+    for k in range(1, NX):
+        greet(gx, gy, x_peer(k))
+
     loads = [
         pltpu.make_async_copy(rhs_hbm.at[:, pl.ds(0, LANES)], rhs_a, load_sem.at[0]),
         pltpu.make_async_copy(inv_hbm, inv_all.at[gz], load_sem.at[1]),
@@ -59,22 +70,6 @@
     ]
     for n in (5, 0, 1, 2, 4, 3, 6, 7):
         loads[n].start()
-
-    barrier = pltpu.get_barrier_semaphore()
-
-    def greet(px, py, pz):
-        pl.semaphore_signal(barrier, inc=1, device_id=(px, py, pz), device_id_type=MESH)
-
-    def x_peer(k):
-        return lax.rem(gz + 2 * k, n_gz)
-
-    for step in Y_ORDER:
-        greet(gx, lax.rem(gy + step, n_gy), gz)
-    for turn in G_FAR + G_NEAR:
-        greet(lax.bitwise_xor(gx, turn), gy, gz)
-    greet(gx, gy, z_peer)
-    for k in range(1, NX):
-        greet(gx, gy, x_peer(k))
 
     def turn_of(j):
         away = (j + 1) // 2
@@ -167,28 +162,25 @@
             for r in range(32):
                 front[h][pl.ds(base + r, 1), :] = got[h][pl.ds(recv_order[base + r], 1), :]
 
-    whole = (inv_all, low_all, par_all)
+    def piece(w, place):
+        if w < 2:
+            return (inv_all, low_all)[w].at[place]
+        return par_all.at[place, w - 2]
+
+    def factor_copy(w, place, send_sem, recv_sem, to):
+        return pltpu.make_async_remote_copy(
+            src_ref=piece(w, place), dst_ref=piece(w, place), send_sem=send_sem, recv_sem=recv_sem,
+            device_id=(gx, gy, to), device_id_type=MESH,
+        )
 
     def z_copy(w):
-        return pltpu.make_async_remote_copy(
-            src_ref=whole[w].at[gz], dst_ref=whole[w].at[gz],
-            send_sem=z_send.at[w], recv_sem=z_recv.at[w],
-            device_id=(gx, gy, z_peer), device_id_type=MESH,
-        )
+        return factor_copy(w, gz, z_send.at[w], z_recv.at[w], z_peer)
 
     def x_copy(w, k):
-        return pltpu.make_async_remote_copy(
-            src_ref=whole[w].at[gz], dst_ref=whole[w].at[gz],
-            send_sem=x_send.at[w, k - 1], recv_sem=x_recv.at[w, k - 1],
-            device_id=(gx, gy, x_peer(k)), device_id_type=MESH,
-        )
+        return factor_copy(w, gz, x_send.at[w, k - 1], x_recv.at[w, k - 1], x_peer(k))
 
     def f_copy(w, k):
-        return pltpu.make_async_remote_copy(
-            src_ref=whole[w].at[z_peer], dst_ref=whole[w].at[z_peer],
-            send_sem=f_send.at[w, k - 1], recv_sem=f_recv.at[w, k - 1],
-            device_id=(gx, gy, x_peer(k)), device_id_type=MESH,
-        )
+        return factor_copy(w, z_peer, f_send.at[w, k - 1], f_recv.at[w, k - 1], x_peer(k))
 
     def share_along_x(w):
         for k in (1, 3, 2):
@@ -216,14 +208,33 @@
         mask = jnp.broadcast_to(mask[None], tiles)
         return jnp.where(mask, new.reshape(tiles), old.reshape(tiles)).reshape(shape)
 
+    def split(x):
+        high = x.astype(jnp.bfloat16)
+        return high, (x - high.astype(jnp.float32)).astype(jnp.bfloat16)
+
+    def split_factor(whole, high, low):
+        rows = whole.shape[2]
+        for f in range(whole.shape[1]):
+            for g in range(n_gz):
+                at = pl.ds(g * rows, rows)
+                high[f, at, :], low[f, at, :] = split(whole[g, f])
+
+    def product(a_high, a_low, b):
+        high, low = split(b)
+        both = jnp.dot(
+            a_high, jnp.concatenate([high, low], axis=1), preferred_element_type=jnp.float32
+        )
+        rest = jnp.dot(a_low, high, preferred_element_type=jnp.float32)
+        return both[:, :LANES] + both[:, LANES:] + rest
+
     def leaf_stage(h):
         cols = pl.ds(h * LANES, LANES)
         take_rows(h)
         for l in range(LEAF_DEV):
             rows = pl.ds(l * PIV, PIV)
-            sol = dot(inv_all[:, l].reshape(PIV, PIV), front[h][rows, :])
+            sol = product(inv_hi[l], inv_lo[l], front[h][rows, :])
             out[rows, cols] = sol
-            upd[h, l] = dot(low_all[:, l].reshape(PIV, PIV), sol)
+            upd[h, l] = product(low_hi[l], low_lo[l], sol)
         firsts = [splat(gy * LEAF_DEV + l, 0) for l in range(LEAF_DEV)]
         for step in Y_ORDER + (0,):
             there = lax.rem(gy + step, n_gy)
@@ -272,28 +283,12 @@
             ).wait()
             absorb(h, source)
 
-    def split(x):
-        high = x.astype(jnp.bfloat16)
-        return high, (x - high.astype(jnp.float32)).astype(jnp.bfloat16)
-
-    def split_parents():
-        for p in range(PAR_DEV):
-            rows = par_all.shape[2]
-            for g in range(n_gz):
-                at = pl.ds(g * rows, rows)
-                par_hi[p, at, :], par_lo[p, at, :] = split(par_all[g, p])
-
     def parent_stage(h):
         absorb_all(h)
         cols = pl.ds(h * LANES, LANES)
         for p in range(PAR_DEV):
             rows = pl.ds(LEAF_DEV * PIV + p * 4 * BLK, 4 * BLK)
-            high, low = split(front[h][rows, :])
-            both = jnp.dot(
-                par_hi[p], jnp.concatenate([high, low], axis=1), preferred_element_type=jnp.float32
-            )
-            rest = jnp.dot(par_lo[p], high, preferred_element_type=jnp.float32)
-            out[rows, cols] = both[:, :LANES] + both[:, LANES:] + rest
+            out[rows, cols] = product(par_hi[p], par_lo[p], front[h][rows, :])
 
     loads[1].wait()
     loads[2].wait()
@@ -304,8 +299,8 @@
     z_copy(0).start()
     z_copy(1).start()
     pick_and_send_along_y(0, far, 0)
-    for w in range(3):
-        share_along_x(w)
+    share_along_x(0)
+    share_along_x(1)
     pick_and_send_along_y(0, near, 1)
     loads[3].wait()
     pick_rows(1, far)
@@ -317,28 +312,35 @@
     send_along_y(1, far, 0)
     forward_factor(0)
     forward_factor(1)
+    share_along_x(2)
+    share_along_x(3)
     await_y(0, 1)
     send_along_gx(0, G_NEAR, 1)
     send_along_y(1, near, 1)
     keep_own(0)
+    await_factor(0)
+    split_factor(inv_all, inv_hi, inv_lo)
+    await_factor(1)
+    split_factor(low_all, low_hi, low_lo)
     await_gx(0)
     await_y(1, 0)
     send_along_gx(1, G_FAR, 0)
-    await_factor(0)
-    await_factor(1)
     leaf_stage(0)
     await_y(1, 1)
     send_along_gx(1, G_NEAR, 1)
     keep_own(1)
     await_gx(1)
     z_copy(2).start()
+    z_copy(3).start()
     leaf_stage(1)
     forward_factor(2)
+    forward_factor(3)
     await_factor(2)
-    split_parents()
+    await_factor(3)
+    split_factor(par_all, par_hi, par_lo)
     parent_stage(0)
     parent_stage(1)
-    for w in range(3):
+    for w in range(4):
         z_copy(w).wait_send()
         for k in range(1, NX):
             x_copy(w, k).wait_send()
@@ -356,6 +358,7 @@
     any_space = pl.BlockSpec(memory_space=pl.ANY)
     half = pltpu.VMEM((rows, LANES), f32)
     lots = pltpu.VMEM((n_gx, rows // n_gx, LANES), f32)
+    leaf_half = pltpu.VMEM((LEAF_DEV, PIV, PIV), jnp.bfloat16)
     dma = pltpu.SemaphoreType.DMA
     return pl.pallas_call(
         functools.partial(kernel, n_gx, n_gy, n_gz),
@@ -372,13 +375,14 @@
             pltpu.VMEM((n_gy, PIV, LANES), f32),
             pltpu.VMEM((n_gy, PIV, LANES), f32),
             pltpu.VMEM((n_gy, PIV, LANES), f32),
+            leaf_half, leaf_half, leaf_half, leaf_half,
             pltpu.VMEM((PAR_DEV, 4 * BLK, 4 * BLK), jnp.bfloat16),
             pltpu.VMEM((PAR_DEV, 4 * BLK, 4 * BLK), jnp.bfloat16),
             pltpu.SMEM((rows,), jnp.int32),
             pltpu.SMEM((rows,), jnp.int32),
             pltpu.SMEM(update_target.shape[::-1], jnp.int32),
-            dma((8,)), dma((3,)), dma((3,)),
-            dma((3, NX - 1)), dma((3, NX - 1)), dma((3, NX - 1)), dma((3, NX - 1)),
+            dma((8,)), dma((4,)), dma((4,)),
+            dma((4, NX - 1)), dma((4, NX - 1)), dma((4, NX - 1)), dma((4, NX - 1)),
             dma((2,)), dma((2, 2)), dma((2,)), dma((2, 2)), dma((2,)), dma((2, n_gy)),
         ],
         compiler_params=pltpu.CompilerParams(

time: 110 us -> 108 us (0.982)
  Pallas kernels: 108 us -> 106 us
    pallas_call x1, Pallas kernels: 108 us -> 106 us  [body(): pl.pallas_call(functools.partial(kernel, n_gx, n_gy, n_gz), out_shape=plt...]
where the time goes in v4:
time: 108 us; the launch traced here: 107 us
  Pallas kernels  106 us (98%)
  local copies, waits for them, and re-layouts  1.32 us (1%)
    pallas_call x1, Pallas kernels, body(): pl.pallas_call(functools.partial(kernel, n_gx, n_gy, n_gz), out_shape=plt...  106 us

profile of v4, /device:TPU:1, one launch (start us, length us, event | category | flops | bytes accessed | tf_op | source)
XLA Modules:
  0.0 107.4 jit_solution(2214237079950180318)
XLA Ops:
  0.0 106.1 %forward_solve.1 = f32[2048,256]{1,0:T(8,128)S(1)} custom-call(s32[2048]{0:T(1024)} %bitcast.3, s32[2048]{0:T(1024)} %bitcast.4, s32[2,32]{1,0:T(2,128)} %bitcast.5, f32[2048,256]{1,0:T(8,128)} %rhs_hbm.1, f32[4,32,256]{2,1,0:T(8,128)} %inv_hbm.1, f32[4,32,256]{2,1,0:T(8,128)} %low_hbm.1, f32[2,64,512]{2,1,0:T(8,128)} %par_hbm.1), custom_call_target="tpu_custom_call" | custom-call | tf_op jit(solution)/shard_map/forward_solve/pallas_call | solution.py:363
  106.1 1.3 %copy.9 = f32[2048,256]{1,0:T(8,128)} copy(f32[2048,256]{1,0:T(8,128)S(1)} %forward_solve.1) | data formatting | bytes 4194304

commit v5 on v4

--- a/solution.py
+++ b/solution.py
@@ -155,8 +155,8 @@
     def bulk(view, sem):
         pltpu.make_async_copy(view, view, sem).wait()
 
-    def take_rows(h):
-        @pl.loop(0, front[h].shape[0] // 32)
+    def take_rows(h, first, last):
+        @pl.loop(first // 32, last // 32)
         def _(c):
             base = pl.multiple_of(c * 32, 32)
             for r in range(32):
@@ -229,7 +229,7 @@
 
     def leaf_stage(h):
         cols = pl.ds(h * LANES, LANES)
-        take_rows(h)
+        take_rows(h, 0, LEAF_DEV * PIV)
         for l in range(LEAF_DEV):
             rows = pl.ds(l * PIV, PIV)
             sol = product(inv_hi[l], inv_lo[l], front[h][rows, :])
@@ -254,6 +254,7 @@
                 send_sem=upd_send.at[h], recv_sem=upd_recv.at[h, step],
                 device_id=(gx, lax.rem(gy + step, n_gy), gz), device_id_type=MESH,
             ).start()
+        take_rows(h, LEAF_DEV * PIV, front[h].shape[0])
 
     def absorb(h, source):
         zeros = jnp.zeros((BLK, LANES), jnp.float32)

time: 108 us -> 108 us (level)
  no operation moved by 1% of the time
where the time goes in v5:
time: 108 us; the launch traced here: 107 us
  Pallas kernels  106 us (98%)
  local copies, waits for them, and re-layouts  1.32 us (1%)
    pallas_call x1, Pallas kernels, body(): pl.pallas_call(functools.partial(kernel, n_gx, n_gy, n_gz), out_shape=plt...  106 us

profile of v5, /device:TPU:1, one launch (start us, length us, event | category | flops | bytes accessed | tf_op | source)
XLA Modules:
  0.0 107.4 jit_solution(13920746790937233782)
XLA Ops:
  0.0 106.1 %forward_solve.1 = f32[2048,256]{1,0:T(8,128)S(1)} custom-call(s32[2048]{0:T(1024)} %bitcast.3, s32[2048]{0:T(1024)} %bitcast.4, s32[2,32]{1,0:T(2,128)} %bitcast.5, f32[2048,256]{1,0:T(8,128)} %rhs_hbm.1, f32[4,32,256]{2,1,0:T(8,128)} %inv_hbm.1, f32[4,32,256]{2,1,0:T(8,128)} %low_hbm.1, f32[2,64,512]{2,1,0:T(8,128)} %par_hbm.1), custom_call_target="tpu_custom_call" | custom-call | tf_op jit(solution)/shard_map/forward_solve/pallas_call | solution.py:364
  106.1 1.3 %copy.9 = f32[2048,256]{1,0:T(8,128)} copy(f32[2048,256]{1,0:T(8,128)S(1)} %forward_solve.1) | data formatting | bytes 4194304
